TPU v7x, 128 devices: a whole 4x4x4 slice. The times are simulated.
128 devices in a mesh: layer: 32 (over x_hi, y, z), cuts: 4 (over x_lo, core).
Axes of the slice: x: 4 (x_hi: 2, x_lo: 2; x = x_hi * 2 + x_lo), y: 4, z: 4, core: 2. Of those that a mesh axis runs over, the one named last changes fastest.
Arguments:
- resid: bfloat16 [512, 2, 16384], P(None, None, 'cuts'), may hold values from -6 to 6
- enc_weight: bfloat16 [2, 16384, 8192], P(None, 'cuts', 'layer'), may hold values from -0.03125 to 0.03125
- enc_bias: float32 [8192], P('layer'), may hold values from -1 to 1
- dec_weight: bfloat16 [8192, 2, 16384], P('layer', None, 'cuts'), may hold values from -0.09375 to 0.09375
- dec_bias: float32 [2, 16384], P(None, 'cuts'), may hold values from -1 to 1
Outputs:
- enc_grad: bfloat16 [2, 16384, 8192], P(None, 'cuts', 'layer')
- dec_grad: bfloat16 [8192, 2, 16384], P('layer', None, 'cuts')
All inputs are finite; a program needn't handle non-finite values.
Results may differ from a plain program's by a relative error of at most 0.012.
Values may be sent and summed in bfloat16 or wider, within the bound.
A program may use at most 128 MiB of HBM per device.

v0:
```python
import math

import jax
import jax.numpy as jnp
from jax import lax
from jax.sharding import PartitionSpec as P


def copy_for_each(x, axis):
    copies = jnp.broadcast_to(x, (lax.axis_size(axis), *x.shape))
    return lax.all_to_all(copies, axis, split_axis=0, concat_axis=0, tiled=True)


def taken_together(x, axis):
    everything = copy_for_each(x, axis)
    return jnp.sum(everything, axis=0)


def filled_up(lines, size):
    spare = -len(lines) % size
    return jnp.pad(lines, [(0, spare)] + [(0, 0)] * (lines.ndim - 1))


def sum_by_parts(x, axis):
    lines = x.reshape(-1, *x.shape[1:][-1:])
    padded = filled_up(lines, lax.axis_size(axis))
    own = lax.psum_scatter(padded, axis, scatter_dimension=0, tiled=True)
    whole = lax.all_gather(own, axis, axis=0, tiled=True)
    return whole[: len(lines)].reshape(x.shape)


def per_device(resid, enc_weight, enc_bias, dec_weight, dec_bias):
    rows = resid.shape[0]
    local = resid.reshape(rows, -1)
    width = local.shape[1]
    encoder = enc_weight.reshape(width, -1)
    feats = encoder.shape[1]
    decoder = dec_weight.reshape(feats, width)
    offset = dec_bias.reshape(-1)
    scale = 1.0 / math.sqrt(rows)
    groups = lax.axis_size("layer")
    partial_sum = jnp.dot(local, encoder, preferred_element_type=jnp.float32)
    z_local = taken_together(partial_sum, "cuts") + enc_bias[None, :]
    act = jnp.maximum(z_local, 0.0).astype(jnp.bfloat16)
    share = rows // groups
    block = act
    recon = lax.psum_scatter(
        jnp.dot(block, decoder, preferred_element_type=jnp.float32),
        "layer",
        scatter_dimension=0,
        tiled=True,
    )
    mine = lax.axis_index("layer") * share
    own_rows = lax.dynamic_slice_in_dim(local, mine, share, 0)
    err = (recon + offset[None, :] - own_rows.astype(jnp.float32)).astype(jnp.bfloat16)
    piece = lax.all_gather(err, "layer", axis=0, tiled=True)
    block = act
    grad = lax.dot_general(
        block, piece, (((0,), (0,)), ((), ())), preferred_element_type=jnp.float32
    )
    values = lax.dot_general(
        piece, decoder, (((1,), (1,)), ((), ())), preferred_element_type=jnp.float32
    )
    dact = values
    grad, dact = (grad, dact)
    dec_grad = (grad * scale).astype(jnp.bfloat16)
    back = sum_by_parts(dact, "cuts")
    masked = jnp.where(z_local > 0, back * scale, 0.0).astype(jnp.bfloat16)
    enc_full = lax.dot_general(
        local, masked, (((0,), (0,)), ((), ())), preferred_element_type=jnp.float32
    )
    enc_grad = enc_full.astype(jnp.bfloat16).reshape(enc_weight.shape)
    return (enc_grad, dec_grad.reshape(dec_weight.shape))


def solution(mesh):
    placed = (
        P(None, None, "cuts"),
        P(None, "cuts", "layer"),
        P("layer"),
        P("layer", None, "cuts"),
        P(None, "cuts"),
    )
    return jax.shard_map(
        per_device,
        mesh=mesh,
        in_specs=placed,
        out_specs=(P(None, "cuts", "layer"), P("layer", None, "cuts")),
        check_vma=False,
    )
```

profile of v0, /device:TPU:1, one launch (start us, length us, event | category | flops | bytes accessed | tf_op | source)
XLA Modules:
  0.0 445.2 jit_solution(11260148202417527209)
XLA Ops:
  7.2 9.3 %fusion.4 = f32[512,256]{1,0:T(8,128)S(1)} fusion(bf16[2,4096,256]{2,1,0:T(8,128)(2,1)} %param.6, bf16[512,2,4096]{2,1,0:T(2,128)(2,1)} %param.5), kind=kOutput, calls=%fused_computation.6 | convolution fusion | flops 2147483648 | bytes 13107200 | tf_op jit(solution)/shard_map/dot_general | solution.py:42
  16.5 0.0 copy-start
  16.5 1.5 broadcast_in_dim.6
  18.0 5.0 %all-to-all-start = ((f32[4,512,256]{2,1,0:T(8,128)}), f32[4,512,256]{2,1,0:T(8,128)S(1)}, u32[]{:S(2)}, u32[]{:S(2)}) async-start(f32[4,512,256]{2,1,0:T(8,128)} %broadcast_in_dim.6), calls=%async_computation | async-start | bytes 4194304 | tf_op jit(solution)/shard_map/all_to_all | solution.py:11
  22.9 0.0 reduce-scatter.3.cloned.1.call-start
  22.9 8.7 %copy.12 = bf16[32,8,2,4096]{3,1,2,0:T(8,128)(2,1)} copy(bf16[32,8,2,4096]{3,2,1,0:T(2,128)(2,1)} %bitcast.22) | data formatting | bytes 8388608
  31.6 16.0 %all-to-all-done = f32[4,512,256]{2,1,0:T(8,128)S(1)} async-done(((f32[4,512,256]{2,1,0:T(8,128)}), f32[4,512,256]{2,1,0:T(8,128)S(1)}, u32[]{:S(2)}, u32[]{:S(2)}) %all-to-all-start) | async-done | bytes 2097184 | tf_op jit(solution)/shard_map/all_to_all | solution.py:11
  47.6 0.2 reduce_sum.9
  47.8 0.0 copy-done
  47.8 10.3 %fusion.10 = f32[512,8192]{1,0:T(8,128)} fusion(bf16[256,8192]{1,0:T(8,128)(2,1)} %bitcast.19, f32[512,256]{1,0:T(8,128)S(1)} %reduce_sum.9, f32[256]{0:T(256)S(1)} %copy-done), kind=kOutput, calls=%fused_computation.13 | convolution fusion | flops 2147876864 | bytes 21496832 | tf_op jit(solution)/shard_map/dot_general | solution.py:48
  58.1 0.0 reduce-scatter.3.cloned.1.call-update
  58.1 0.3 all-gather.2.cloned.1.call-start
  58.4 0.0 copy-start.1
  58.4 16.2 %copy.14 = bf16[64,8,2,4096]{3,1,2,0:T(8,128)(2,1)} copy(bf16[64,8,2,4096]{3,2,1,0:T(2,128)(2,1)} %bitcast.21) | data formatting | bytes 16777216
  74.6 0.0 copy-done.1
  74.6 194.2 %reduce-scatter.3.cloned.1.call-done = f32[16,8192]{1,0:T(8,128)} async-done(((f32[512,8192]{1,0:T(8,128)}), f32[16,8192]{1,0:T(8,128)}) %reduce-scatter.3.cloned.1.call-update) | async-done | bytes 524304 | tf_op jit(solution)/shard_map/reduce_scatter | solution.py:47
  268.8 1.9 subtract_convert_fusion
  270.7 0.0 all-gather.2.cloned.1.call-update
  270.7 0.3 reduce-scatter.5.cloned.1.call-start
  271.0 120.5 %all-gather.2.cloned.1.call-done = bf16[512,8192]{1,0:T(8,128)(2,1)} async-done(((bf16[16,8192]{1,0:T(8,128)(2,1)}), bf16[512,8192]{1,0:T(8,128)(2,1)}) %all-gather.2.cloned.1.call-update) | async-done | bytes 8388624 | tf_op jit(solution)/shard_map/all_gather | solution.py:56
  391.6 7.8 %fusion.15 = f32[512,256]{1,0:T(8,128)} fusion(bf16[512,8192]{1,0:T(8,128)(2,1)} %all-gather.2.cloned.1.call-done, bf16[256,8192]{1,0:T(8,128)(2,1)} %bitcast.20), kind=kOutput, calls=%fused_computation.18 | convolution fusion | flops 2147483648 | bytes 13107200 | tf_op jit(solution)/shard_map/dot_general | solution.py:61
  399.3 0.0 reduce-scatter.5.cloned.1.call-update
  399.4 7.8 %fusion = bf16[256,8192]{1,0:T(8,128)(2,1)} fusion(bf16[512,8192]{1,0:T(8,128)(2,1)} %all-gather.2.cloned.1.call-done, f32[512,256]{1,0:T(8,128)S(1)} %reduce_sum.9, f32[256]{0:T(256)S(1)} %copy-done), kind=kOutput, calls=%fused_computation.1 | convolution fusion | flops 2152071168 | bytes 13108224 | tf_op jit(solution)/shard_map/dot_general | solution.py:58
  407.2 7.8 %reshape.22 = bf16[256,2,4096]{2,1,0:T(2,128)(2,1)} reshape(bf16[256,8192]{1,0:T(8,128)(2,1)} %fusion) | data formatting | bytes 8388608 | tf_op jit(solution)/shard_map/reshape | solution.py:73
  415.0 2.1 reduce-scatter.5.cloned.1.call-done
  417.1 7.5 %all_gather.7 = f32[512,256]{1,0:T(8,128)S(1)} all-gather(f32[128,256]{1,0:T(8,128)} %reduce-scatter.5.cloned.1.call-done), channel_id=1, replica_groups=mesh['layer'=32,'cuts'=4] {'cuts'}, dimensions={0}, use_global_device_ids=true | all-gather | bytes 655360 | tf_op jit(solution)/shard_map/all_gather | solution.py:28
  424.5 7.8 %fusion.1 = bf16[8192,256]{0,1:T(8,128)(2,1)} fusion(bf16[512,8192]{1,0:T(8,128)(2,1)} %bitcast.18, f32[512,256]{1,0:T(8,128)S(1)} %all_gather.7, f32[512,256]{1,0:T(8,128)S(1)} %reduce_sum.9, f32[256]{0:T(256)S(1)} %copy-done), kind=kOutput, calls=%fused_computation.3 | convolution fusion | flops 2150236160 | bytes 13632512 | tf_op jit(solution)/shard_map/dot_general | solution.py:69
  432.3 6.4 %copy.11 = bf16[8192,256]{1,0:T(8,128)(2,1)} copy(bf16[8192,256]{0,1:T(8,128)(2,1)} %fusion.1) | data formatting | bytes 8388608
  (1 shorter events, 0.0 us)
Async XLA Ops:
  16.5 31.3 %copy-start = (f32[256]{0:T(256)S(1)}, f32[256]{0:T(256)}, u32[]{:S(2)}) copy-start(f32[256]{0:T(256)} %param.7) | copy-start | bytes 3076
  18.0 29.7 %all-to-all-start = ((f32[4,512,256]{2,1,0:T(8,128)}), f32[4,512,256]{2,1,0:T(8,128)S(1)}, u32[]{:S(2)}, u32[]{:S(2)}) async-start(f32[4,512,256]{2,1,0:T(8,128)} %broadcast_in_dim.6), calls=%async_computation | async-start | bytes 4194304 | tf_op jit(solution)/shard_map/all_to_all | solution.py:11
  22.9 245.9 %reduce-scatter.3.cloned.1.call-start = ((), (), s32[]{:S(2)}) async-start(), calls=%async_computation.3 | async-start | bytes 17301504 | tf_op jit(solution)/shard_map/reduce_scatter | solution.py:47
  58.1 333.4 %all-gather.2.cloned.1.call-start = ((), (), s32[]{:S(2)}) async-start(), calls=%async_computation.4 | async-start | bytes 8650752 | tf_op jit(solution)/shard_map/all_gather | solution.py:56
  58.4 16.2 %copy-start.1 = (f32[2,4096]{1,0:T(2,128)S(1)}, f32[2,4096]{1,0:T(2,128)}, u32[]{:S(2)}) copy-start(f32[2,4096]{1,0:T(2,128)} %param.9) | copy-start | bytes 98308
  270.7 146.3 %reduce-scatter.5.cloned.1.call-start = ((), (), s32[]{:S(2)}) async-start(), calls=%async_computation.5 | async-start | bytes 655360 | tf_op jit(solution)/shard_map/reduce_scatter | solution.py:27
Sparse Core Ops, SparseCore 0:
  58.2 210.5 reduce-scatter.2
  272.6 118.9 all-gather.1
  399.5 17.5 reduce-scatter.4
where the time goes:
time: 446 us; the launch traced here: 445 us
  waiting for transfers between devices  333 us (75%)
  matrix products  42.9 us (10%)
  local copies, waits for them, and re-layouts  40.6 us (9%)
  between operations  13.8 us (3%)
  blocking collectives  7.48 us (2%)
  starting transfers between devices  5.52 us (1%)
    reduce_scatter x1, waiting for transfers between devices, per_device(): lax.psum_scatter(jnp.dot(block, decoder, preferred_element_type=jnp.float...  194 us
    all_gather x1, waiting for transfers between devices, per_device(): piece = lax.all_gather(err, 'layer', axis=0, tiled=True)  121 us
    unnamed x8, local copies, waits for them, and re-layouts  31.3 us
    all_to_all x1, waiting for transfers between devices, copy_for_each(): return lax.all_to_all(copies, axis, split_axis=0, concat_axis=0, tiled=True)  16 us
    dot_general x1, matrix products, per_device(): jnp.dot(block, decoder, preferred_element_type=jnp.float32)  10.3 us
    dot_general x1, matrix products, per_device(): partial_sum = jnp.dot(local, encoder, preferred_element_type=jnp.float32)  9.32 us
  transfers between devices with their start and end apart: 4, of which 4 were waited for; matrix products, arithmetic and copies ran while one was open for 9% of the time, Pallas kernels for 0%

commit v1 on v0

v1 whole, which is shorter than its diff:
```python
import functools
import math

import jax
import jax.numpy as jnp
from jax import lax
from jax.experimental import pallas as pl
from jax.experimental.pallas import tpu as pltpu
from jax.sharding import PartitionSpec as P

MESH = pl.DeviceIdType.MESH
F32 = jnp.float32
BF16 = jnp.bfloat16

CHUNKS = 8
BW = 256
RING = 4

Z = 0
RS1_FAR, RS1_NEAR, RS2_FAR, RS2_NEAR = 3, 7, 11, 15
XSUM = 19
AG2_NEAR, AG2_FAR, AG1_NEAR, AG1_FAR = 20, 24, 28, 32
DACT = 36
MESSAGES = 39
LOCAL = 6


def exchange_kernel(
    resid, enc, enc_bias, dec, dec_bias,
    act_out, dz_out, err_out, plain_out,
    enc_v, dec_raw, dec_v, raw, plain, own_resid, zs, zf, act_v,
    rec, far1, near1, far2, near2, xs, xr, err, own_d, ds, dr,
    send_sems, recv_sems, copy_sems, err_sems, plain_sems,
):
    layer, cut = lax.axis_index("layer"), lax.axis_index("cuts")
    x_hi, py, pz = layer // 16, (layer // 4) % 4, layer % 4
    rows = resid.shape[0]
    n = CHUNKS
    tile = rows // n
    half = tile // 2
    width = resid.shape[2]
    scale = 1.0 / math.sqrt(rows)

    def at(hi, y, z):
        return (hi * 16 + y * 4 + z, cut)

    def hop(axis, by):
        if axis == 0:
            return at(x_hi, (py + by) % 4, pz)
        return at(x_hi, py, (pz + by) % 4)

    across = at(1 - x_hi, py, pz)

    def mate(k):
        low = (cut + (k + 1) % 2) % 2
        high = (cut // 2 + (k + 1) // 2) % 2
        return high * 2 + low

    first = (py, pz)
    second = (pz, py)

    def send(m, c, src, dst, device):
        pltpu.make_async_remote_copy(
            src_ref=src, dst_ref=dst, send_sem=send_sems.at[c, m], recv_sem=recv_sems.at[c, m],
            device_id=device, device_id_type=MESH,
        ).start()

    def copy_of(m, c, ref):
        return pltpu.make_async_remote_copy(
            src_ref=ref, dst_ref=ref, send_sem=send_sems.at[c, m], recv_sem=recv_sems.at[c, m],
            device_id=across, device_id_type=MESH,
        )

    def landed(m, c, ref):
        copy_of(m, c, ref).wait_recv()

    def load_raw(c):
        return pltpu.make_async_copy(
            resid.at[pl.ds(c * tile, tile)], raw.at[c % 2], copy_sems.at[c % 2]
        )

    load_enc = pltpu.make_async_copy(enc, enc_v, copy_sems.at[2])
    load_dec = pltpu.make_async_copy(dec, dec_raw, copy_sems.at[3])

    def save_plain(c):
        return pltpu.make_async_copy(
            plain.at[c % 2], plain_out.at[:, pl.ds(c * tile, tile)], plain_sems.at[c % 2]
        )

    def save_err(c):
        return pltpu.make_async_copy(
            err.at[c], err_out.at[:, :, pl.ds(c * tile, tile)], err_sems.at[c]
        )

    load_raw(0).start()
    load_enc.start()
    load_dec.start()
    load_raw(1).start()

    barrier = pltpu.get_barrier_semaphore()
    peers = [hop(a, by) for a in (0, 1) for by in (1, 3)] + [across]
    peers += [(layer, mate(k)) for k in range(3)]
    for peer in peers:
        pl.semaphore_signal(barrier, inc=1, device_id=peer, device_id_type=MESH)
    pl.semaphore_wait(barrier, len(peers))

    def encode(c):
        load_raw(c).wait()
        slot = c % 2

        @pl.when(c >= 2)
        def _():
            save_plain(c - 2).wait()

        def split(i, carry):
            s = pl.ds(pl.multiple_of(i * 16, 16), 16)
            for l in range(2):
                plain[slot, l, s, :] = raw[slot, s, l, :]
            return carry

        lax.fori_loop(0, tile // 16, split, 0)

        @pl.when(c + 2 < n)
        def _():
            load_raw(c + 2).start()

        save_plain(c).start()

        @pl.when(c == 0)
        def _():
            load_enc.wait()

        def mul(i, acc):
            for l in range(2):
                for u in range(2):
                    k = pl.ds(pl.multiple_of((2 * i + u) * BW, BW), BW)
                    acc += jnp.dot(plain[slot, l, :, k], enc_v[l, k, :], preferred_element_type=F32)
            return acc

        acc = lax.fori_loop(0, width // (2 * BW), mul, jnp.zeros((tile, enc.shape[2]), F32))
        zs[c, cut] = acc
        for k in range(3):
            send(Z + k, c, zs.at[c, cut], zs.at[c, cut], (layer, mate(k)))
        for h in range(2):
            b = (4 * first[h] + second[h]) * BW
            own_resid[c, h] = plain[slot, h, :, pl.ds(pl.multiple_of(b, BW), BW)]

    def split_dec():
        load_dec.wait()

        def split(i, carry):
            s = pl.ds(pl.multiple_of(i * 16, 16), 16)
            for l in range(2):
                dec_v[l, s, :] = dec_raw[s, l, :]
            return carry

        lax.fori_loop(0, dec.shape[0] // 16, split, 0)

    def decode(c):
        for k in range(3):
            landed(Z + k, c, zs.at[c, mate(k)])
        z = zs[c, 0] + zs[c, 1] + zs[c, 2] + zs[c, 3] + enc_bias[...]
        zf[c] = z
        act = jnp.maximum(z, 0.0).astype(BF16)
        act_v[c] = act

        def mul(i, carry):
            for h in range(2):
                q = (first[h] + 2 + i) % RING
                for j in range(4):
                    b = 4 * q + j
                    cols = pl.ds(pl.multiple_of(b * BW, BW), BW)
                    rec[c, h, b] = jnp.dot(
                        act, dec_v[h, :, cols], preferred_element_type=F32
                    ).astype(BF16)
            return carry

        mul(0, 0)
        for h in range(2):
            q = (first[h] + 2) % RING
            for d in range(2):
                send(
                    RS1_FAR + 2 * h + d, c,
                    rec.at[c, h, pl.ds(4 * q, 4), pl.ds(d * half, half)], far1.at[c, h, d],
                    hop(h, 1 + 2 * d),
                )
        lax.fori_loop(1, 4, mul, 0)

    def rs1_relay(c):
        for h in range(2):
            for d in range(2):
                landed(RS1_FAR + 2 * h + d, c, far1.at[c, h, d])
                q = (first[h] + 1 + 2 * d) % RING
                rs = slice(d * half, (d + 1) * half)
                for k in range(4):
                    mine = rec[c, h, 4 * q + k, rs, :].astype(F32)
                    rec[c, h, 4 * q + k, rs, :] = (mine + far1[c, h, d, k].astype(F32)).astype(BF16)
                send(
                    RS1_NEAR + 2 * h + d, c, rec.at[c, h, pl.ds(4 * q, 4)], near1.at[c, h, d],
                    hop(h, 1 + 2 * d),
                )

    def rs1_sum(c):
        for h in range(2):
            for d in range(2):
                landed(RS1_NEAR + 2 * h + d, c, near1.at[c, h, d])
            p, q = first[h], (second[h] + 2) % RING
            for k in range(4):
                total = rec[c, h, 4 * p + k].astype(F32) + near1[c, h, 0, k].astype(F32)
                rec[c, h, 4 * p + k] = (total + near1[c, h, 1, k].astype(F32)).astype(BF16)
            for d in range(2):
                send(
                    RS2_FAR + 2 * h + d, c, rec.at[c, h, 4 * p + q, pl.ds(d * half, half)],
                    far2.at[c, h, d], hop(1 - h, 1 + 2 * d),
                )

    def rs2_relay(c):
        for h in range(2):
            for d in range(2):
                landed(RS2_FAR + 2 * h + d, c, far2.at[c, h, d])
                b = 4 * first[h] + (second[h] + 1 + 2 * d) % RING
                rs = slice(d * half, (d + 1) * half)
                mine = rec[c, h, b, rs, :].astype(F32)
                rec[c, h, b, rs, :] = (mine + far2[c, h, d].astype(F32)).astype(BF16)
                send(
                    RS2_NEAR + 2 * h + d, c, rec.at[c, h, b], near2.at[c, h, d],
                    hop(1 - h, 1 + 2 * d),
                )

    def rs2_sum(c):
        for h in range(2):
            for d in range(2):
                landed(RS2_NEAR + 2 * h + d, c, near2.at[c, h, d])
            b = 4 * first[h] + second[h]
            total = rec[c, h, b].astype(F32) + near2[c, h, 0].astype(F32)
            xs[c, h] = (total + near2[c, h, 1].astype(F32)).astype(BF16)
        send(XSUM, c, xs.at[c], xr.at[c], across)

    def error(c):
        landed(XSUM, c, xr.at[c])
        for h in range(2):
            b = 4 * first[h] + second[h]
            cols = pl.ds(pl.multiple_of(b * BW, BW), BW)
            recon = xs[c, h].astype(F32) + xr[c, h].astype(F32)
            value = recon + dec_bias[h : h + 1, cols] - own_resid[c, h].astype(F32)
            err[c, h, b] = value.astype(BF16)
            for d in range(2):
                send(
                    AG2_NEAR + 2 * h + d, c, err.at[c, h, b], err.at[c, h, b],
                    hop(1 - h, 1 + 2 * d),
                )

    def ag2_relay(c):
        for h in range(2):
            for d in range(2):
                b = 4 * first[h] + (second[h] + 3 + 2 * d) % RING
                landed(AG2_NEAR + 2 * h + d, c, err.at[c, h, b])
                part = err.at[c, h, b, pl.ds(d * half, half)]
                send(AG2_FAR + 2 * h + d, c, part, part, hop(1 - h, 1 + 2 * d))

    def ag1_start(c):
        for h in range(2):
            b = 4 * first[h] + (second[h] + 2) % RING
            for d in range(2):
                landed(AG2_FAR + 2 * h + d, c, err.at[c, h, b, pl.ds(d * half, half)])
            piece = err.at[c, h, pl.ds(4 * first[h], 4)]
            for d in range(2):
                send(AG1_NEAR + 2 * h + d, c, piece, piece, hop(h, 1 + 2 * d))

    def ag1_relay(c):
        for h in range(2):
            for d in range(2):
                q = (first[h] + 3 + 2 * d) % RING
                landed(AG1_NEAR + 2 * h + d, c, err.at[c, h, pl.ds(4 * q, 4)])
                part = err.at[c, h, pl.ds(4 * q, 4), pl.ds(d * half, half)]
                send(AG1_FAR + 2 * h + d, c, part, part, hop(h, 1 + 2 * d))

    def back(c):
        for h in range(2):
            q = (first[h] + 2) % RING
            for d in range(2):
                landed(
                    AG1_FAR + 2 * h + d, c, err.at[c, h, pl.ds(4 * q, 4), pl.ds(d * half, half)]
                )
        save_err(c).start()

        def mul(i, acc):
            for h in range(2):
                for j in range(4):
                    b = 4 * i + j
                    cols = pl.ds(pl.multiple_of(b * BW, BW), BW)
                    acc += lax.dot_general(
                        err[c, h, b], dec_v[h, :, cols], (((1,), (1,)), ((), ())),
                        preferred_element_type=F32,
                    )
            return acc

        acc = lax.fori_loop(0, 4, mul, jnp.zeros((tile, dec.shape[0]), F32))
        own_d[c] = acc
        ds[c] = acc.astype(BF16)
        for k in range(3):
            send(DACT + k, c, ds.at[c], dr.at[c, k], (layer, mate(k)))

    def mask(c):
        for k in range(3):
            landed(DACT + k, c, dr.at[c, k])
        total = own_d[c] + dr[c, 0].astype(F32) + dr[c, 1].astype(F32) + dr[c, 2].astype(F32)
        dz_out[c] = jnp.where(zf[c] > 0, total * scale, 0.0).astype(BF16)
        act_out[c] = act_v[c]

    stages = [
        encode, decode, rs1_relay, rs1_sum, rs2_relay, rs2_sum, error, ag2_relay, ag1_start,
        ag1_relay, back, mask,
    ]

    def step(t, carry):
        for lag in reversed(range(len(stages))):
            c = t - lag

            @pl.when((c >= 0) & (c < n))
            def _():
                stages[lag](c)

            if lag == 0:

                @pl.when(t == 0)
                def _():
                    split_dec()

        return carry

    lax.fori_loop(0, n + len(stages) - 1, step, 0)

    def finish(c, carry):
        for k in range(3):
            copy_of(Z + k, c, zs.at[c, cut]).wait_send()
            copy_of(DACT + k, c, ds.at[c]).wait_send()
        for i in range(4):
            h, d = i // 2, i % 2
            copy_of(RS1_FAR + i, c, far1.at[c, h, d]).wait_send()
            copy_of(RS1_NEAR + i, c, near1.at[c, h, d]).wait_send()
            copy_of(RS2_FAR + i, c, far2.at[c, h, d]).wait_send()
            copy_of(RS2_NEAR + i, c, near2.at[c, h, d]).wait_send()
            copy_of(AG2_NEAR + i, c, near2.at[c, h, d]).wait_send()
            copy_of(AG2_FAR + i, c, far2.at[c, h, d]).wait_send()
            copy_of(AG1_NEAR + i, c, near1.at[c, h, d]).wait_send()
            copy_of(AG1_FAR + i, c, far1.at[c, h, d]).wait_send()
        copy_of(XSUM, c, xs.at[c]).wait_send()
        save_err(c).wait()
        return carry

    lax.fori_loop(0, n, finish, 0)
    save_plain(n - 2).wait()
    save_plain(n - 1).wait()


def exchange(resid, enc, enc_bias, dec, dec_bias):
    rows, _, width = resid.shape
    feats = enc.shape[2]
    n, tile = CHUNKS, rows // CHUNKS
    half, blocks = tile // 2, width // BW
    anyspace = pl.BlockSpec(memory_space=pl.ANY)
    vmem = pl.BlockSpec(memory_space=pltpu.VMEM)
    return pl.pallas_call(
        exchange_kernel,
        out_shape=(
            jax.ShapeDtypeStruct((n, tile, feats), BF16),
            jax.ShapeDtypeStruct((n, tile, feats), BF16),
            jax.ShapeDtypeStruct((2, blocks, rows, BW), BF16),
            jax.ShapeDtypeStruct((2, rows, width), BF16),
        ),
        in_specs=[anyspace, anyspace, vmem, anyspace, vmem],
        out_specs=(vmem, vmem, anyspace, anyspace),
        scratch_shapes=[
            pltpu.VMEM((2, width, feats), BF16),
            pltpu.VMEM((feats, 2, width), BF16),
            pltpu.VMEM((2, feats, width), BF16),
            pltpu.VMEM((2, tile, 2, width), BF16),
            pltpu.VMEM((2, 2, tile, width), BF16),
            pltpu.VMEM((n, 2, tile, BW), BF16),
            pltpu.VMEM((n, 4, tile, feats), F32),
            pltpu.VMEM((n, tile, feats), F32),
            pltpu.VMEM((n, tile, feats), BF16),
            pltpu.VMEM((n, 2, blocks, tile, BW), BF16),
            pltpu.VMEM((n, 2, 2, 4, half, BW), BF16),
            pltpu.VMEM((n, 2, 2, 4, tile, BW), BF16),
            pltpu.VMEM((n, 2, 2, half, BW), BF16),
            pltpu.VMEM((n, 2, 2, tile, BW), BF16),
            pltpu.VMEM((n, 2, tile, BW), BF16),
            pltpu.VMEM((n, 2, tile, BW), BF16),
            pltpu.VMEM((n, 2, blocks, tile, BW), BF16),
            pltpu.VMEM((n, tile, feats), F32),
            pltpu.VMEM((n, tile, feats), BF16),
            pltpu.VMEM((n, 3, tile, feats), BF16),
            pltpu.SemaphoreType.DMA((n, MESSAGES)),
            pltpu.SemaphoreType.DMA((n, MESSAGES)),
            pltpu.SemaphoreType.DMA((4,)),
            pltpu.SemaphoreType.DMA((n,)),
            pltpu.SemaphoreType.DMA((2,)),
        ],
        compiler_params=pltpu.CompilerParams(
            collective_id=0, has_side_effects=True, vmem_limit_bytes=60 * 2**20
        ),
        name="exchange",
    )(resid, enc, enc_bias.reshape(1, feats), dec, dec_bias)


def grads_kernel(scale, act, dz, err, plain, enc_grad, dec_grad, act_t, dz_t):
    @pl.when(pl.program_id(0) == 0)
    def _():
        act_t[...] = act[...].T
        dz_t[...] = dz[...].T

    for h in range(2):
        grad = jnp.dot(act_t[...], err[h, 0], preferred_element_type=F32) * scale
        dec_grad[:, h, :] = grad.astype(BF16)
        flipped = jnp.dot(dz_t[...], plain[h], preferred_element_type=F32)
        enc_grad[h] = flipped.astype(BF16).T


def grads(act, dz, err, plain):
    _, rows, width = plain.shape
    feats = act.shape[1]
    full = pl.BlockSpec((rows, feats), lambda b: (0, 0))
    return pl.pallas_call(
        functools.partial(grads_kernel, 1.0 / math.sqrt(rows)),
        grid=(width // BW,),
        out_shape=(
            jax.ShapeDtypeStruct((2, width, feats), BF16),
            jax.ShapeDtypeStruct((feats, 2, width), BF16),
        ),
        in_specs=[
            full,
            full,
            pl.BlockSpec((2, 1, rows, BW), lambda b: (0, b, 0, 0)),
            pl.BlockSpec((2, rows, BW), lambda b: (0, 0, b)),
        ],
        out_specs=(
            pl.BlockSpec((2, BW, feats), lambda b: (0, b, 0)),
            pl.BlockSpec((feats, 2, BW), lambda b: (0, 0, b)),
        ),
        scratch_shapes=[pltpu.VMEM((feats, rows), BF16), pltpu.VMEM((feats, rows), BF16)],
        name="grads",
    )(act, dz, err, plain)


def per_device(resid, enc_weight, enc_bias, dec_weight, dec_bias):
    rows = resid.shape[0]
    act, dz, err, plain = exchange(resid, enc_weight, enc_bias, dec_weight, dec_bias)
    return grads(act.reshape(rows, -1), dz.reshape(rows, -1), err, plain)


def solution(mesh):
    placed = (
        P(None, None, "cuts"),
        P(None, "cuts", "layer"),
        P("layer"),
        P("layer", None, "cuts"),
        P(None, "cuts"),
    )
    return jax.shard_map(
        per_device,
        mesh=mesh,
        in_specs=placed,
        out_specs=(P(None, "cuts", "layer"), P("layer", None, "cuts")),
        check_vma=False,
    )
```

time: 446 us -> 179 us (0.40)
  waiting for transfers between devices: 333 us -> 0 us
  Pallas kernels: 0 us -> 177 us
  matrix products: 42.9 us -> 0 us
  local copies, waits for them, and re-layouts: 40.6 us -> 0 us
  between operations: 13.8 us -> 0.64 us
  blocking collectives: 7.48 us -> 0 us
  starting transfers between devices: 5.52 us -> 0 us
    reduce_scatter x2 -> x0, waiting for transfers between devices: 196 us -> none  [the longest x1 194 us: per_device(): lax.psum_scatter(jnp.dot(block, decoder, preferred_element_type=jnp.float...]
    pallas_call x0 -> x2, Pallas kernels: none -> 177 us  [the longest x1 159 us: exchange(): pl.pallas_call(exchange_kernel, out_shape=(jax.ShapeDtypeStruct((n, tile,...]
    all_gather x1 -> x0, waiting for transfers between devices: 121 us -> none  [per_device(): piece = lax.all_gather(err, 'layer', axis=0, tiled=True)]
    dot_general x5 -> x0, matrix products: 42.9 us -> none  [the longest x1 10.3 us: per_device(): jnp.dot(block, decoder, preferred_element_type=jnp.float32)]
    unnamed x8 -> x0, local copies, waits for them, and re-layouts: 31.3 us -> none
    all_to_all x1 -> x0, waiting for transfers between devices: 16 us -> none  [copy_for_each(): return lax.all_to_all(copies, axis, split_axis=0, concat_axis=0, tiled=True)]
    reshape x1 -> x0, local copies, waits for them, and re-layouts: 7.81 us -> none  [per_device(): return (enc_grad, dec_grad.reshape(dec_weight.shape))]
    all_gather x1 -> x0, blocking collectives: 7.48 us -> none  [sum_by_parts(): whole = lax.all_gather(own, axis, axis=0, tiled=True)]
  transfers between devices with their start and end apart: 4 -> 0, of which waited for: 4 -> 0; matrix products, arithmetic and copies ran while one was open for 9% -> 0% of each run, Pallas kernels for 0% -> 0%
where the time goes in v1:
time: 179 us; the launch traced here: 178 us
  Pallas kernels  177 us (99%)
    pallas_call x1, Pallas kernels, exchange(): pl.pallas_call(exchange_kernel, out_shape=(jax.ShapeDtypeStruct((n, tile,...  159 us
    pallas_call x1, Pallas kernels, grads(): pl.pallas_call(functools.partial(grads_kernel, 1.0 / math.sqrt(rows)), gr...  17.9 us

profile of v1, /device:TPU:1, one launch (start us, length us, event | category | flops | bytes accessed | tf_op | source)
XLA Modules:
  0.0 178.0 jit_solution(18161684976363455559)
XLA Ops:
  0.6 159.5 %exchange.1 = (bf16[8,64,256]{2,1,0:T(8,128)(2,1)}, bf16[8,64,256]{2,1,0:T(8,128)(2,1)}, bf16[2,16,512,256]{3,2,1,0:T(8,128)(2,1)}, bf16[2,512,4096]{2,1,0:T(8,128)(2,1)}) custom-call(bf16[512,2,4096]{2,1,0:T(2,128)(2,1)} %resid.1, bf16[2,4096,256]{2,1,0:T(8,128)(2,1)} %enc.1, f32[1,256]{1,0:T(1,128)} %bitcast.5, bf16[256,2,4096]{2,1,0:T(2,128)(2,1)} %dec.1, ...), custom_call_target="tpu_custom_call" | custom-call | tf_op jit(solution)/shard_map/exchange/pallas_call | solution.py:364
  160.1 17.9 %grads.1 = (bf16[2,4096,256]{2,1,0:T(8,128)(2,1)}, bf16[256,2,4096]{2,1,0:T(2,128)(2,1)}) custom-call(bf16[512,256]{1,0:T(8,128)(2,1)} %bitcast.3, bf16[512,256]{1,0:T(8,128)(2,1)} %bitcast.4, bf16[2,16,512,256]{3,2,1,0:T(8,128)(2,1)} %get-tuple-element.8.err, bf16[2,512,4096]{2,1,0:T(8,128)(2,1)} %get-tuple-element.9.plain), custom_call_target="tpu_custom_call" | custom-call | tf_op jit(solution)/shard_map/grads/pallas_call | solution.py:425

commit v2 on v1

--- a/solution.py
+++ b/solution.py
@@ -114,8 +114,7 @@
 
         def split(i, carry):
             s = pl.ds(pl.multiple_of(i * 16, 16), 16)
-            for l in range(2):
-                plain[slot, l, s, :] = raw[slot, s, l, :]
+            plain[slot, :, s, :] = jnp.swapaxes(raw[slot, s], 0, 1)
             return carry
 
         lax.fori_loop(0, tile // 16, split, 0)
@@ -150,8 +149,7 @@
 
         def split(i, carry):
             s = pl.ds(pl.multiple_of(i * 16, 16), 16)
-            for l in range(2):
-                dec_v[l, s, :] = dec_raw[s, l, :]
+            dec_v[:, s, :] = jnp.swapaxes(dec_raw[s], 0, 1)
             return carry
 
         lax.fori_loop(0, dec.shape[0] // 16, split, 0)
@@ -313,8 +311,10 @@
         ag1_relay, back, mask,
     ]
 
+    ORDER = range(len(stages))
+
     def step(t, carry):
-        for lag in reversed(range(len(stages))):
+        for lag in ORDER:
             c = t - lag
 
             @pl.when((c >= 0) & (c < n))
@@ -412,10 +412,12 @@
         dz_t[...] = dz[...].T
 
     for h in range(2):
-        grad = jnp.dot(act_t[...], err[h, 0], preferred_element_type=F32) * scale
-        dec_grad[:, h, :] = grad.astype(BF16)
-        flipped = jnp.dot(dz_t[...], plain[h], preferred_element_type=F32)
-        enc_grad[h] = flipped.astype(BF16).T
+        for u in range(err.shape[1]):
+            s = slice(u * BW, (u + 1) * BW)
+            grad = jnp.dot(act_t[...], err[h, u], preferred_element_type=F32) * scale
+            dec_grad[:, h, s] = grad.astype(BF16)
+            flipped = jnp.dot(dz_t[...], plain[h, :, s], preferred_element_type=F32)
+            enc_grad[h, s] = flipped.astype(BF16).T
 
 
 def grads(act, dz, err, plain):
@@ -424,7 +426,7 @@
     full = pl.BlockSpec((rows, feats), lambda b: (0, 0))
     return pl.pallas_call(
         functools.partial(grads_kernel, 1.0 / math.sqrt(rows)),
-        grid=(width // BW,),
+        grid=(width // (4 * BW),),
         out_shape=(
             jax.ShapeDtypeStruct((2, width, feats), BF16),
             jax.ShapeDtypeStruct((feats, 2, width), BF16),
@@ -432,12 +434,12 @@
         in_specs=[
             full,
             full,
-            pl.BlockSpec((2, 1, rows, BW), lambda b: (0, b, 0, 0)),
-            pl.BlockSpec((2, rows, BW), lambda b: (0, 0, b)),
+            pl.BlockSpec((2, 4, rows, BW), lambda b: (0, b, 0, 0)),
+            pl.BlockSpec((2, rows, 4 * BW), lambda b: (0, 0, b)),
         ],
         out_specs=(
-            pl.BlockSpec((2, BW, feats), lambda b: (0, b, 0)),
-            pl.BlockSpec((feats, 2, BW), lambda b: (0, 0, b)),
+            pl.BlockSpec((2, 4 * BW, feats), lambda b: (0, b, 0)),
+            pl.BlockSpec((feats, 2, 4 * BW), lambda b: (0, 0, b)),
         ),
         scratch_shapes=[pltpu.VMEM((feats, rows), BF16), pltpu.VMEM((feats, rows), BF16)],
         name="grads",

time: 179 us -> 131 us (0.73)
  Pallas kernels: 177 us -> 130 us
    pallas_call x1, Pallas kernels: 159 us -> 118 us  [exchange(): pl.pallas_call(exchange_kernel, out_shape=(jax.ShapeDtypeStruct((n, tile,...]
    pallas_call x1, Pallas kernels: 17.9 us -> 12.5 us  [grads(): pl.pallas_call(functools.partial(grads_kernel, 1.0 / math.sqrt(rows)), gr...]
where the time goes in v2:
time: 131 us
  Pallas kernels  130 us (99%)
    pallas_call x1, Pallas kernels, exchange(): pl.pallas_call(exchange_kernel, out_shape=(jax.ShapeDtypeStruct((n, tile,...  118 us
    pallas_call x1, Pallas kernels, grads(): pl.pallas_call(functools.partial(grads_kernel, 1.0 / math.sqrt(rows)), gr...  12.5 us

profile of v2, /device:TPU:1, one launch (start us, length us, event | category | flops | bytes accessed | tf_op | source)
XLA Modules:
  0.0 131.0 jit_solution(5367501700923700818)
XLA Ops:
  0.6 117.9 %exchange.1 = (bf16[8,64,256]{2,1,0:T(8,128)(2,1)}, bf16[8,64,256]{2,1,0:T(8,128)(2,1)}, bf16[2,16,512,256]{3,2,1,0:T(8,128)(2,1)}, bf16[2,512,4096]{2,1,0:T(8,128)(2,1)}) custom-call(bf16[512,2,4096]{2,1,0:T(2,128)(2,1)} %resid.1, bf16[2,4096,256]{2,1,0:T(8,128)(2,1)} %enc.1, f32[1,256]{1,0:T(1,128)} %bitcast.5, bf16[256,2,4096]{2,1,0:T(2,128)(2,1)} %dec.1, ...), custom_call_target="tpu_custom_call" | custom-call | tf_op jit(solution)/shard_map/exchange/pallas_call | solution.py:364
  118.5 12.5 %grads.1 = (bf16[2,4096,256]{2,1,0:T(8,128)(2,1)}, bf16[256,2,4096]{2,1,0:T(2,128)(2,1)}) custom-call(bf16[512,256]{1,0:T(8,128)(2,1)} %bitcast.3, bf16[512,256]{1,0:T(8,128)(2,1)} %bitcast.4, bf16[2,16,512,256]{3,2,1,0:T(8,128)(2,1)} %get-tuple-element.8.err, bf16[2,512,4096]{2,1,0:T(8,128)(2,1)} %get-tuple-element.9.plain), custom_call_target="tpu_custom_call" | custom-call | tf_op jit(solution)/shard_map/grads/pallas_call | solution.py:427

commit v3 on v2

--- a/solution.py
+++ b/solution.py
@@ -1,4 +1,3 @@
-import functools
 import math
 
 import jax
@@ -14,6 +13,8 @@
 
 CHUNKS = 8
 BW = 256
+PART = 1024
+VMEM_LIMIT = 97 * 2**19
 RING = 4
 
 Z = 0
@@ -22,15 +23,14 @@
 AG2_NEAR, AG2_FAR, AG1_NEAR, AG1_FAR = 20, 24, 28, 32
 DACT = 36
 MESSAGES = 39
-LOCAL = 6
 
 
 def exchange_kernel(
     resid, enc, enc_bias, dec, dec_bias,
-    act_out, dz_out, err_out, plain_out,
-    enc_v, dec_raw, dec_v, raw, plain, own_resid, zs, zf, act_v,
+    enc_v, dec_grad,
+    dec_raw, dec_v, raw, plain, own_resid, zs, zf, act_v, dz_v, act_t, dz_t,
     rec, far1, near1, far2, near2, xs, xr, err, own_d, ds, dr,
-    send_sems, recv_sems, copy_sems, err_sems, plain_sems,
+    send_sems, recv_sems, copy_sems, out_sems, bias_v, dec_bias_v,
 ):
     layer, cut = lax.axis_index("layer"), lax.axis_index("cuts")
     x_hi, py, pz = layer // 16, (layer // 4) % 4, layer % 4
@@ -79,42 +79,36 @@
             resid.at[pl.ds(c * tile, tile)], raw.at[c % 2], copy_sems.at[c % 2]
         )
 
-    load_enc = pltpu.make_async_copy(enc, enc_v, copy_sems.at[2])
+    def load_enc(i):
+        part = pl.ds(pl.multiple_of(i * (width // 2), width // 2), width // 2)
+        return pltpu.make_async_copy(enc.at[:, part], enc_v.at[:, part], copy_sems.at[4 + i])
+
     load_dec = pltpu.make_async_copy(dec, dec_raw, copy_sems.at[3])
 
-    def save_plain(c):
-        return pltpu.make_async_copy(
-            plain.at[c % 2], plain_out.at[:, pl.ds(c * tile, tile)], plain_sems.at[c % 2]
-        )
-
-    def save_err(c):
-        return pltpu.make_async_copy(
-            err.at[c], err_out.at[:, :, pl.ds(c * tile, tile)], err_sems.at[c]
-        )
+    def save_dec(i):
+        part = pl.ds(pl.multiple_of(i * PART, PART), PART)
+        return pltpu.make_async_copy(dec_raw.at[:, :, part], dec_grad.at[:, :, part], out_sems.at[i])
+
+    load_bias = pltpu.make_async_copy(enc_bias, bias_v, copy_sems.at[2])
+    load_dec_bias = pltpu.make_async_copy(dec_bias, dec_bias_v, copy_sems.at[6])
 
     load_raw(0).start()
-    load_enc.start()
-    load_dec.start()
-    load_raw(1).start()
+    load_enc(0).start()
+    load_enc(1).start()
 
     barrier = pltpu.get_barrier_semaphore()
     peers = [hop(a, by) for a in (0, 1) for by in (1, 3)] + [across]
     peers += [(layer, mate(k)) for k in range(3)]
     for peer in peers:
         pl.semaphore_signal(barrier, inc=1, device_id=peer, device_id_type=MESH)
-    pl.semaphore_wait(barrier, len(peers))
-
-    def encode(c):
+    def encode_own(c):
         load_raw(c).wait()
-        slot = c % 2
-
-        @pl.when(c >= 2)
-        def _():
-            save_plain(c - 2).wait()
+        here = pl.ds(pl.multiple_of(c * tile, tile), tile)
 
         def split(i, carry):
             s = pl.ds(pl.multiple_of(i * 16, 16), 16)
-            plain[slot, :, s, :] = jnp.swapaxes(raw[slot, s], 0, 1)
+            to = pl.ds(pl.multiple_of(c * tile + i * 16, 16), 16)
+            plain[:, to, :] = jnp.swapaxes(raw[c % 2, s], 0, 1)
             return carry
 
         lax.fori_loop(0, tile // 16, split, 0)
@@ -123,29 +117,46 @@
         def _():
             load_raw(c + 2).start()
 
-        save_plain(c).start()
+        per = width // (2 * BW)
+
+        def mul(i, acc):
+            @pl.when(c == 0)
+            def _():
+                load_enc(i).wait()
+
+            for l in range(2):
+                for u in range(per):
+                    k = pl.ds(pl.multiple_of((per * i + u) * BW, BW), BW)
+                    acc += jnp.dot(plain[l, here, k], enc_v[l, k, :], preferred_element_type=F32)
+            return acc
+
+        acc = lax.fori_loop(0, 2, mul, jnp.zeros((tile, enc.shape[2]), F32))
 
         @pl.when(c == 0)
         def _():
-            load_enc.wait()
-
-        def mul(i, acc):
-            for l in range(2):
-                for u in range(2):
-                    k = pl.ds(pl.multiple_of((2 * i + u) * BW, BW), BW)
-                    acc += jnp.dot(plain[slot, l, :, k], enc_v[l, k, :], preferred_element_type=F32)
-            return acc
-
-        acc = lax.fori_loop(0, width // (2 * BW), mul, jnp.zeros((tile, enc.shape[2]), F32))
+            load_raw(1).start()
+            load_dec.start()
+            load_bias.start()
+            load_dec_bias.start()
+
         zs[c, cut] = acc
+
+    def encode(c):
+        @pl.when(c > 0)
+        def _():
+            encode_own(c)
+
         for k in range(3):
             send(Z + k, c, zs.at[c, cut], zs.at[c, cut], (layer, mate(k)))
+        here = pl.ds(pl.multiple_of(c * tile, tile), tile)
         for h in range(2):
             b = (4 * first[h] + second[h]) * BW
-            own_resid[c, h] = plain[slot, h, :, pl.ds(pl.multiple_of(b, BW), BW)]
+            own_resid[c, h] = plain[h, here, pl.ds(pl.multiple_of(b, BW), BW)]
 
     def split_dec():
         load_dec.wait()
+        load_bias.wait()
+        load_dec_bias.wait()
 
         def split(i, carry):
             s = pl.ds(pl.multiple_of(i * 16, 16), 16)
@@ -157,7 +168,7 @@
     def decode(c):
         for k in range(3):
             landed(Z + k, c, zs.at[c, mate(k)])
-        z = zs[c, 0] + zs[c, 1] + zs[c, 2] + zs[c, 3] + enc_bias[...]
+        z = zs[c, 0] + zs[c, 1] + zs[c, 2] + zs[c, 3] + bias_v[...]
         zf[c] = z
         act = jnp.maximum(z, 0.0).astype(BF16)
         act_v[c] = act
@@ -182,7 +193,8 @@
                     rec.at[c, h, pl.ds(4 * q, 4), pl.ds(d * half, half)], far1.at[c, h, d],
                     hop(h, 1 + 2 * d),
                 )
-        lax.fori_loop(1, 4, mul, 0)
+        for i in range(1, 4):
+            mul(i, 0)
 
     def rs1_relay(c):
         for h in range(2):
@@ -240,7 +252,7 @@
             b = 4 * first[h] + second[h]
             cols = pl.ds(pl.multiple_of(b * BW, BW), BW)
             recon = xs[c, h].astype(F32) + xr[c, h].astype(F32)
-            value = recon + dec_bias[h : h + 1, cols] - own_resid[c, h].astype(F32)
+            value = recon + dec_bias_v[h : h + 1, cols] - own_resid[c, h].astype(F32)
             err[c, h, b] = value.astype(BF16)
             for d in range(2):
                 send(
@@ -280,12 +292,10 @@
                 landed(
                     AG1_FAR + 2 * h + d, c, err.at[c, h, pl.ds(4 * q, 4), pl.ds(d * half, half)]
                 )
-        save_err(c).start()
-
         def mul(i, acc):
             for h in range(2):
-                for j in range(4):
-                    b = 4 * i + j
+                for j in range(8):
+                    b = 8 * i + j
                     cols = pl.ds(pl.multiple_of(b * BW, BW), BW)
                     acc += lax.dot_general(
                         err[c, h, b], dec_v[h, :, cols], (((1,), (1,)), ((), ())),
@@ -293,7 +303,7 @@
                     )
             return acc
 
-        acc = lax.fori_loop(0, 4, mul, jnp.zeros((tile, dec.shape[0]), F32))
+        acc = lax.fori_loop(0, 2, mul, jnp.zeros((tile, dec.shape[0]), F32))
         own_d[c] = acc
         ds[c] = acc.astype(BF16)
         for k in range(3):
@@ -303,35 +313,9 @@
         for k in range(3):
             landed(DACT + k, c, dr.at[c, k])
         total = own_d[c] + dr[c, 0].astype(F32) + dr[c, 1].astype(F32) + dr[c, 2].astype(F32)
-        dz_out[c] = jnp.where(zf[c] > 0, total * scale, 0.0).astype(BF16)
-        act_out[c] = act_v[c]
-
-    stages = [
-        encode, decode, rs1_relay, rs1_sum, rs2_relay, rs2_sum, error, ag2_relay, ag1_start,
-        ag1_relay, back, mask,
-    ]
-
-    ORDER = range(len(stages))
-
-    def step(t, carry):
-        for lag in ORDER:
-            c = t - lag
-
-            @pl.when((c >= 0) & (c < n))
-            def _():
-                stages[lag](c)
-
-            if lag == 0:
-
-                @pl.when(t == 0)
-                def _():
-                    split_dec()
-
-        return carry
-
-    lax.fori_loop(0, n + len(stages) - 1, step, 0)
-
-    def finish(c, carry):
+        dz_v[c] = jnp.where(zf[c] > 0, total * scale, 0.0).astype(BF16)
+
+    def finish(c):
         for k in range(3):
             copy_of(Z + k, c, zs.at[c, cut]).wait_send()
             copy_of(DACT + k, c, ds.at[c]).wait_send()
@@ -346,12 +330,72 @@
             copy_of(AG1_NEAR + i, c, near1.at[c, h, d]).wait_send()
             copy_of(AG1_FAR + i, c, far1.at[c, h, d]).wait_send()
         copy_of(XSUM, c, xs.at[c]).wait_send()
-        save_err(c).wait()
+
+    def make_dec_grad():
+        act_t[...] = act_v[...].reshape(rows, -1).T
+
+        def mul(i, carry):
+            for u in range(PART // BW):
+                b = (PART // BW) * i + u
+                cols = pl.ds(pl.multiple_of(b * BW, BW), BW)
+                both = []
+                for h in range(2):
+                    tall = jnp.concatenate([err[c, h, b] for c in range(n)], axis=0)
+                    grad = jnp.dot(act_t[...], tall, preferred_element_type=F32) * scale
+                    both.append(grad.astype(BF16))
+                dec_raw[:, :, cols] = jnp.swapaxes(jnp.stack(both), 0, 1)
+            save_dec(i).start()
+            return carry
+
+        lax.fori_loop(0, width // PART, mul, 0)
+
+    def make_enc_grad():
+        dz_t[...] = dz_v[...].reshape(rows, -1).T
+
+        def mul(i, carry):
+            for u in range(PART // BW):
+                b = (PART // BW) * i + u
+                cols = pl.ds(pl.multiple_of(b * BW, BW), BW)
+                for h in range(2):
+                    flipped = jnp.dot(dz_t[...], plain[h, :, cols], preferred_element_type=F32)
+                    enc_v[h, cols, :] = flipped.astype(BF16).T
+            return carry
+
+        lax.fori_loop(0, width // PART, mul, 0)
+
+    stages = [
+        encode, decode, rs1_relay, rs1_sum, rs2_relay, rs2_sum, error, ag2_relay, ag1_start,
+        ag1_relay, back, mask, finish,
+    ]
+
+    ORDER = range(len(stages))
+
+    def step(t, carry):
+        for lag in ORDER:
+            c = t - lag
+
+            @pl.when((c >= 0) & (c < n))
+            def _():
+                stages[lag](c)
+
+            if lag == 0:
+
+                @pl.when(t == 0)
+                def _():
+                    split_dec()
+
+        @pl.when(t == n - 1 + stages.index(back))
+        def _():
+            make_dec_grad()
+
         return carry
 
-    lax.fori_loop(0, n, finish, 0)
-    save_plain(n - 2).wait()
-    save_plain(n - 1).wait()
+    encode_own(0)
+    pl.semaphore_wait(barrier, len(peers))
+    lax.fori_loop(0, n + len(stages) - 1, step, 0)
+    make_enc_grad()
+    for i in range(width // PART):
+        save_dec(i).wait()
 
 
 def exchange(resid, enc, enc_bias, dec, dec_bias):
@@ -359,28 +403,28 @@
     feats = enc.shape[2]
     n, tile = CHUNKS, rows // CHUNKS
     half, blocks = tile // 2, width // BW
-    anyspace = pl.BlockSpec(memory_space=pl.ANY)
+    hbm = pl.BlockSpec(memory_space=pltpu.HBM)
     vmem = pl.BlockSpec(memory_space=pltpu.VMEM)
     return pl.pallas_call(
         exchange_kernel,
         out_shape=(
-            jax.ShapeDtypeStruct((n, tile, feats), BF16),
-            jax.ShapeDtypeStruct((n, tile, feats), BF16),
-            jax.ShapeDtypeStruct((2, blocks, rows, BW), BF16),
-            jax.ShapeDtypeStruct((2, rows, width), BF16),
+            jax.ShapeDtypeStruct((2, width, feats), BF16),
+            jax.ShapeDtypeStruct((feats, 2, width), BF16),
         ),
-        in_specs=[anyspace, anyspace, vmem, anyspace, vmem],
-        out_specs=(vmem, vmem, anyspace, anyspace),
+        in_specs=[hbm] * 5,
+        out_specs=(vmem, hbm),
         scratch_shapes=[
-            pltpu.VMEM((2, width, feats), BF16),
             pltpu.VMEM((feats, 2, width), BF16),
             pltpu.VMEM((2, feats, width), BF16),
             pltpu.VMEM((2, tile, 2, width), BF16),
-            pltpu.VMEM((2, 2, tile, width), BF16),
+            pltpu.VMEM((2, rows, width), BF16),
             pltpu.VMEM((n, 2, tile, BW), BF16),
             pltpu.VMEM((n, 4, tile, feats), F32),
             pltpu.VMEM((n, tile, feats), F32),
             pltpu.VMEM((n, tile, feats), BF16),
+            pltpu.VMEM((n, tile, feats), BF16),
+            pltpu.VMEM((feats, rows), BF16),
+            pltpu.VMEM((feats, rows), BF16),
             pltpu.VMEM((n, 2, blocks, tile, BW), BF16),
             pltpu.VMEM((n, 2, 2, 4, half, BW), BF16),
             pltpu.VMEM((n, 2, 2, 4, tile, BW), BF16),
@@ -394,62 +438,20 @@
             pltpu.VMEM((n, 3, tile, feats), BF16),
             pltpu.SemaphoreType.DMA((n, MESSAGES)),
             pltpu.SemaphoreType.DMA((n, MESSAGES)),
-            pltpu.SemaphoreType.DMA((4,)),
-            pltpu.SemaphoreType.DMA((n,)),
-            pltpu.SemaphoreType.DMA((2,)),
+            pltpu.SemaphoreType.DMA((7,)),
+            pltpu.SemaphoreType.DMA((width // PART,)),
+            pltpu.VMEM((1, feats), F32),
+            pltpu.VMEM((2, width), F32),
         ],
         compiler_params=pltpu.CompilerParams(
-            collective_id=0, has_side_effects=True, vmem_limit_bytes=60 * 2**20
+            collective_id=0, has_side_effects=True, vmem_limit_bytes=VMEM_LIMIT
         ),
         name="exchange",
     )(resid, enc, enc_bias.reshape(1, feats), dec, dec_bias)
 
 
-def grads_kernel(scale, act, dz, err, plain, enc_grad, dec_grad, act_t, dz_t):
-    @pl.when(pl.program_id(0) == 0)
-    def _():
-        act_t[...] = act[...].T
-        dz_t[...] = dz[...].T
-
-    for h in range(2):
-        for u in range(err.shape[1]):
-            s = slice(u * BW, (u + 1) * BW)
-            grad = jnp.dot(act_t[...], err[h, u], preferred_element_type=F32) * scale
-            dec_grad[:, h, s] = grad.astype(BF16)
-            flipped = jnp.dot(dz_t[...], plain[h, :, s], preferred_element_type=F32)
-            enc_grad[h, s] = flipped.astype(BF16).T
-
-
-def grads(act, dz, err, plain):
-    _, rows, width = plain.shape
-    feats = act.shape[1]
-    full = pl.BlockSpec((rows, feats), lambda b: (0, 0))
-    return pl.pallas_call(
-        functools.partial(grads_kernel, 1.0 / math.sqrt(rows)),
-        grid=(width // (4 * BW),),
-        out_shape=(
-            jax.ShapeDtypeStruct((2, width, feats), BF16),
-            jax.ShapeDtypeStruct((feats, 2, width), BF16),
-        ),
-        in_specs=[
-            full,
-            full,
-            pl.BlockSpec((2, 4, rows, BW), lambda b: (0, b, 0, 0)),
-            pl.BlockSpec((2, rows, 4 * BW), lambda b: (0, 0, b)),
-        ],
-        out_specs=(
-            pl.BlockSpec((2, 4 * BW, feats), lambda b: (0, b, 0)),
-            pl.BlockSpec((feats, 2, 4 * BW), lambda b: (0, 0, b)),
-        ),
-        scratch_shapes=[pltpu.VMEM((feats, rows), BF16), pltpu.VMEM((feats, rows), BF16)],
-        name="grads",
-    )(act, dz, err, plain)
-
-
 def per_device(resid, enc_weight, enc_bias, dec_weight, dec_bias):
-    rows = resid.shape[0]
-    act, dz, err, plain = exchange(resid, enc_weight, enc_bias, dec_weight, dec_bias)
-    return grads(act.reshape(rows, -1), dz.reshape(rows, -1), err, plain)
+    return exchange(resid, enc_weight, enc_bias, dec_weight, dec_bias)
 
 
 def solution(mesh):

time: 131 us -> 129 us (0.985)
  Pallas kernels: 130 us -> 121 us
  local copies, waits for them, and re-layouts: 0 us -> 7.14 us
    pallas_call x2 -> x1, Pallas kernels: 130 us -> 121 us  [exchange(): pl.pallas_call(exchange_kernel, out_shape=(jax.ShapeDtypeStruct((2, width...]
    unnamed x0 -> x8, local copies, waits for them, and re-layouts: none -> 7.14 us
where the time goes in v3:
time: 129 us; the launch traced here: 128 us
  Pallas kernels  121 us (94%)
  local copies, waits for them, and re-layouts  7.14 us (6%)
    pallas_call x1, Pallas kernels, exchange(): pl.pallas_call(exchange_kernel, out_shape=(jax.ShapeDtypeStruct((2, width...  121 us
    unnamed x8, local copies, waits for them, and re-layouts  7.14 us

profile of v3, /device:TPU:1, one launch (start us, length us, event | category | flops | bytes accessed | tf_op | source)
XLA Modules:
  0.0 128.4 jit_solution(3464228584585841656)
XLA Ops:
  0.6 0.0 copy-start
  0.6 0.7 copy-done
  1.4 0.0 copy-start.1
  1.4 0.7 copy-done.1
  2.1 120.6 %exchange.1 = (bf16[2,4096,256]{2,1,0:T(8,128)(2,1)S(1)}, bf16[256,2,4096]{2,1,0:T(2,128)(2,1)}) custom-call(bf16[512,2,4096]{2,1,0:T(2,128)(2,1)} %resid.1, bf16[2,4096,256]{2,1,0:T(8,128)(2,1)} %enc.1, f32[1,256]{1,0:T(1,128)S(1)} %bitcast.1, bf16[256,2,4096]{2,1,0:T(2,128)(2,1)} %dec.1, f32[2,4096]{1,0:T(2,128)S(1)} %copy-done), custom_call_target="tpu_custom_call" | custom-call | tf_op jit(solution)/shard_map/exchange/pallas_call | solution.py:408
  122.7 0.0 copy-start.2
  122.7 2.1 %copy.9 = bf16[2,4096,256]{2,1,0:T(8,128)(2,1)} copy(bf16[2,4096,256]{2,1,0:T(8,128)(2,1)S(1)} %get-tuple-element.4) | data formatting | bytes 8388608
  124.8 1.6 %copy-done.2 = bf16[256,2,4096]{2,1,0:T(2,128)(2,1)S(1)} copy-done((bf16[256,2,4096]{2,1,0:T(2,128)(2,1)S(1)}, bf16[256,2,4096]{2,1,0:T(2,128)(2,1)}, u32[]{:S(2)}) %copy-start.2) | copy-done | bytes 4194328
  126.4 2.0 %copy.10 = bf16[256,2,4096]{2,1,0:T(2,128)(2,1)} copy(bf16[256,2,4096]{2,1,0:T(2,128)(2,1)S(1)} %copy-done.2) | data formatting | bytes 8388608
Async XLA Ops:
  0.6 0.8 copy-start
  1.4 0.7 copy-start.1
  122.7 3.7 %copy-start.2 = (bf16[256,2,4096]{2,1,0:T(2,128)(2,1)S(1)}, bf16[256,2,4096]{2,1,0:T(2,128)(2,1)}, u32[]{:S(2)}) copy-start(bf16[256,2,4096]{2,1,0:T(2,128)(2,1)} %get-tuple-element.5) | copy-start | bytes 12582916

commit v4 on v3

--- a/solution.py
+++ b/solution.py
@@ -146,7 +146,7 @@
         def _():
             encode_own(c)
 
-        for k in range(3):
+        for k in (1, 2, 0):
             send(Z + k, c, zs.at[c, cut], zs.at[c, cut], (layer, mate(k)))
         here = pl.ds(pl.multiple_of(c * tile, tile), tile)
         for h in range(2):
@@ -306,7 +306,7 @@
         acc = lax.fori_loop(0, 2, mul, jnp.zeros((tile, dec.shape[0]), F32))
         own_d[c] = acc
         ds[c] = acc.astype(BF16)
-        for k in range(3):
+        for k in (1, 2, 0):
             send(DACT + k, c, ds.at[c], dr.at[c, k], (layer, mate(k)))
 
     def mask(c):
@@ -332,8 +332,6 @@
         copy_of(XSUM, c, xs.at[c]).wait_send()
 
     def make_dec_grad():
-        act_t[...] = act_v[...].reshape(rows, -1).T
-
         def mul(i, carry):
             for u in range(PART // BW):
                 b = (PART // BW) * i + u
@@ -383,6 +381,10 @@
                 @pl.when(t == 0)
                 def _():
                     split_dec()
+
+        @pl.when(t == n + stages.index(decode) + 3)
+        def _():
+            act_t[...] = act_v[...].reshape(rows, -1).T
 
         @pl.when(t == n - 1 + stages.index(back))
         def _():

time: 129 us -> 129 us (level)
  no operation moved by 1% of the time
where the time goes in v4:
time: 129 us; the launch traced here: 128 us
  Pallas kernels  120 us (93%)
  local copies, waits for them, and re-layouts  7.14 us (6%)
    pallas_call x1, Pallas kernels, exchange(): pl.pallas_call(exchange_kernel, out_shape=(jax.ShapeDtypeStruct((2, width...  120 us
    unnamed x8, local copies, waits for them, and re-layouts  7.14 us

profile of v4, /device:TPU:1, one launch (start us, length us, event | category | flops | bytes accessed | tf_op | source)
XLA Modules:
  0.0 128.3 jit_solution(14874331734671975467)
XLA Ops:
  0.6 0.0 copy-start
  0.6 0.7 copy-done
  1.4 0.0 copy-start.1
  1.4 0.7 copy-done.1
  2.1 120.5 %exchange.1 = (bf16[2,4096,256]{2,1,0:T(8,128)(2,1)S(1)}, bf16[256,2,4096]{2,1,0:T(2,128)(2,1)}) custom-call(bf16[512,2,4096]{2,1,0:T(2,128)(2,1)} %resid.1, bf16[2,4096,256]{2,1,0:T(8,128)(2,1)} %enc.1, f32[1,256]{1,0:T(1,128)S(1)} %bitcast.1, bf16[256,2,4096]{2,1,0:T(2,128)(2,1)} %dec.1, f32[2,4096]{1,0:T(2,128)S(1)} %copy-done), custom_call_target="tpu_custom_call" | custom-call | tf_op jit(solution)/shard_map/exchange/pallas_call | solution.py:410
  122.6 0.0 copy-start.2
  122.6 2.1 %copy.9 = bf16[2,4096,256]{2,1,0:T(8,128)(2,1)} copy(bf16[2,4096,256]{2,1,0:T(8,128)(2,1)S(1)} %get-tuple-element.4) | data formatting | bytes 8388608
  124.7 1.6 %copy-done.2 = bf16[256,2,4096]{2,1,0:T(2,128)(2,1)S(1)} copy-done((bf16[256,2,4096]{2,1,0:T(2,128)(2,1)S(1)}, bf16[256,2,4096]{2,1,0:T(2,128)(2,1)}, u32[]{:S(2)}) %copy-start.2) | copy-done | bytes 4194328
  126.3 2.0 %copy.10 = bf16[256,2,4096]{2,1,0:T(2,128)(2,1)} copy(bf16[256,2,4096]{2,1,0:T(2,128)(2,1)S(1)} %copy-done.2) | data formatting | bytes 8388608
Async XLA Ops:
  0.6 0.8 copy-start
  1.4 0.7 copy-start.1
  122.6 3.7 %copy-start.2 = (bf16[256,2,4096]{2,1,0:T(2,128)(2,1)S(1)}, bf16[256,2,4096]{2,1,0:T(2,128)(2,1)}, u32[]{:S(2)}) copy-start(bf16[256,2,4096]{2,1,0:T(2,128)(2,1)} %get-tuple-element.5) | copy-start | bytes 12582916
